TPU v7x, 32 devices: a whole 2x2x4 slice. The times are simulated.
32 devices in a mesh: groups: 2 (over y), lon: 16 (over z, x, core).
Axes of the slice: x: 2, y: 2, z: 4, core: 2. Of those that a mesh axis runs over, the one named last changes fastest.
Arguments:
- fields: bfloat16 [4, 24, 192, 192], P('groups', None, 'lon'), parts along dimension 0, may hold values from -6 to 6
- norm_gain: float32 [192], replicated, may hold values from 0.25 to 1.75
- qkv_weight: bfloat16 [192, 576], replicated, may hold values from -2.5 to 2.5
- proj_weight: bfloat16 [192, 192], replicated, may hold values from -0.4375 to 0.4375
- bias_table: float32 [4, 6, 3312], replicated, may hold values from -4 to 4
- bias_index: int32 [144, 144], replicated, may hold values from 0 to 3311
- region_ids: int32 [2, 24], replicated, may hold values from 0 to 2
- mlp_gain: float32 [192], replicated, may hold values from 0.25 to 1.75
- up_weight: bfloat16 [192, 768], replicated, may hold values from -0.4375 to 0.4375
- down_weight: bfloat16 [768, 192], replicated, may hold values from -0.21875 to 0.21875
- merge_gain: float32 [768], replicated, may hold values from 0.25 to 1.75
- merge_weight: bfloat16 [768, 384], replicated, may hold values from -0.21875 to 0.21875
- cotangent: bfloat16 [4, 12, 96, 384], P('groups', None, 'lon'), parts along dimension 0, may hold values from -12 to 12
Outputs:
- merged: bfloat16 [4, 12, 96, 384], P('groups', None, 'lon'), parts along dimension 0
- field_grad: bfloat16 [4, 24, 192, 192], P('groups', None, 'lon'), parts along dimension 0
- qkv_grad: float32 [384, 576], P('groups'), parts along dimension 0
- proj_grad: float32 [384, 192], P('groups'), parts along dimension 0
- up_grad: float32 [384, 768], P('groups'), parts along dimension 0
- down_grad: float32 [1536, 192], P('groups'), parts along dimension 0
- merge_grad: float32 [1536, 384], P('groups'), parts along dimension 0
- table_grad: float32 [8, 6, 3312], P('groups'), parts along dimension 0
There are 2 independent parts, one for each index of `groups`. A program takes and returns all parts, laid end to end along the dimension named above; an argument that names none is the same for every part. Nothing has to cross between parts.
All inputs are finite; a program needn't handle non-finite values.
Results may differ from a plain program's by a relative error of at most 0.019.
The roundings to bfloat16 on the way count: a program that leaves them out, or rounds other values in their place, can miss the bound.
Values may be sent and summed in bfloat16 or wider, within the bound.
A program may use at most 192 MiB of HBM per device.

v0:
```python
import functools

import jax
import jax.numpy as jnp
import numpy as np
from jax import lax
from jax.experimental import pallas as pl
from jax.experimental.pallas import tpu as pltpu
from jax.sharding import PartitionSpec as P

C = 192
MLP = 768
HEADS = 6
HEAD = 32
WZ = 2
WLAT = 6
WLON = 12
HALF = 6
WIN = 144
BPOS = 3312
Z = 2
LAT = 24
TYPES = 4
TH = TYPES * HEADS
LANES = 128
KEYS = 256
RADIX = 256
DIGITS = -(-BPOS // RADIX)
GROUP = WIN // 4
GPAD = 48
ROWS_W = 30 * C
ROWS_T = DIGITS * TH * 2
UNROLL = 4
BF = jnp.bfloat16
F32 = jnp.float32
VMEM = pl.BlockSpec(memory_space=pltpu.VMEM)


def dot(a, b, dims=((1,), (0,))):
    return lax.dot_general(a, b, (dims, ((), ())), preferred_element_type=F32)


NT = ((1,), (1,))
TN = ((0,), (0,))


def bias_kernel(table_ref, digit_ref, lane_ref, out_ref):
    def some_rows(step, carry):
        for u in range(UNROLL):
            i = step * UNROLL + u
            lane = lane_ref[pl.ds(i, 1), :]
            digit = digit_ref[pl.ds(i, 1), :]
            hot = (lax.broadcasted_iota(jnp.int32, (RADIX, KEYS), 0) == lane).astype(BF)
            found = dot(table_ref[...], hot)
            total = jnp.zeros((TH, KEYS), F32)
            for d in range(DIGITS):
                total = jnp.where(digit == d, found[d * TH:(d + 1) * TH], total)
            rows = pl.ds(pl.multiple_of(i * TH, TH), TH)
            out_ref[0, rows, :] = total[:, :LANES]
            out_ref[1, rows, :] = total[:, LANES:]
        return carry

    lax.fori_loop(0, WIN // UNROLL, some_rows, 0)


def norm_parts(values):
    average = jnp.mean(values, axis=-1, keepdims=True)
    centred = values - average
    variance = jnp.mean(centred * centred, axis=-1, keepdims=True)
    scale = lax.rsqrt(variance + 1e-05)
    return centred * scale, scale


def norm_grad(hat, scale, grad_hat):
    first = jnp.mean(grad_hat, axis=-1, keepdims=True)
    second = jnp.mean(grad_hat * hat, axis=-1, keepdims=True)
    return scale * (grad_hat - first - hat * second)


def block_kernel(
    x_ref, ct_ref, bias_ref, regq_ref, regk_ref, digit_ref, lane_ref, perm_ref,
    g1_ref, wqkv_ref, wproj_ref, g2_ref, wup_ref, wdown_ref, gm_ref, wm_ref,
    merged_ref, fgrad_ref, packed_ref,
    triple, prob, mixed, dmixed, dtriple, dscore,
    s_normed, s_dtriple, s_mixed, s_da, s_nmlp, s_du, s_hidden, s_dy, s_merge, s_table,
):
    s_merge[...] = jnp.zeros_like(s_merge)
    triple[...] = jnp.zeros_like(triple)
    root = float(HEAD) ** (-0.5)

    def one_type(t, carry):
        rows = pl.ds(pl.multiple_of(t * WIN, 16), WIN)
        field = x_ref[rows, :].astype(F32)
        hat1, scale1 = norm_parts(field)
        normed = (hat1 * g1_ref[...]).astype(BF)
        s_normed[rows, :] = normed
        triple[0:WIN, :] = dot(normed, wqkv_ref[...]).astype(BF)
        same = regq_ref[t] == regk_ref[t]
        for h in range(HEADS):
            q = triple[0:WIN, h * HEAD:(h + 1) * HEAD]
            k = triple[:, C + h * HEAD:C + (h + 1) * HEAD]
            v = triple[:, 2 * C + h * HEAD:2 * C + (h + 1) * HEAD]
            where_rows = pl.ds(t * HEADS + h, WIN, stride=TH)
            bias = jnp.concatenate(
                [bias_ref[0, where_rows, :], bias_ref[1, where_rows, :]], axis=1
            )
            scores = jnp.where(same, dot(q, k, NT) * root + bias, -1e30)
            weights = jnp.exp(scores - jnp.max(scores, axis=-1, keepdims=True))
            p = weights / jnp.sum(weights, axis=-1, keepdims=True)
            prob[h] = p
            mixed[:, h * HEAD:(h + 1) * HEAD] = dot(p.astype(BF), v).astype(BF)
        mixed_heads = mixed[...]
        s_mixed[rows, :] = mixed_heads
        branch = dot(mixed_heads, wproj_ref[...]).astype(BF).astype(F32)
        after = (field + branch).astype(BF).astype(F32)
        hat2, scale2 = norm_parts(after)
        nmlp = (hat2 * g2_ref[...]).astype(BF)
        s_nmlp[rows, :] = nmlp
        up = dot(nmlp, wup_ref[...])
        cdf = 0.5 * (1.0 + lax.erf(up * np.float32(np.sqrt(0.5))))
        slope = cdf + up * (jnp.exp(-0.5 * up * up) * np.float32(1 / np.sqrt(2 * np.pi)))
        hidden = (up * cdf).astype(BF)
        s_hidden[rows, :] = hidden
        after_mlp = (after + dot(hidden, wdown_ref[...])).astype(BF)

        spread = dot(perm_ref[...], after_mlp)
        parts = [spread[g * GPAD:(g + 1) * GPAD] for g in range(4)]
        average = sum(jnp.sum(p, axis=-1, keepdims=True) for p in parts) / (4 * C)
        parts = [p - average for p in parts]
        variance = sum(jnp.sum(p * p, axis=-1, keepdims=True) for p in parts) / (4 * C)
        scale = lax.rsqrt(variance + 1e-05)
        hats = [p * scale for p in parts]
        ct = ct_ref[t]
        merged = jnp.zeros((GPAD, 2 * C), F32)
        grads = []
        for g in range(4):
            gain = gm_ref[g:g + 1, :]
            weight = wm_ref[g * C:(g + 1) * C, :]
            nm = (hats[g] * gain).astype(BF)
            merged = merged + dot(nm, weight)
            s_merge[g * C:(g + 1) * C, :] += dot(nm, ct, TN)
            grads.append(dot(ct, weight, NT).astype(BF).astype(F32) * gain)
        merged_ref[t] = merged.astype(BF)
        first = sum(jnp.sum(g, axis=-1, keepdims=True) for g in grads) / (4 * C)
        second = sum(
            jnp.sum(g * hat, axis=-1, keepdims=True) for g, hat in zip(grads, hats)
        ) / (4 * C)
        back = jnp.concatenate(
            [scale * (g - first - hat * second) for g, hat in zip(grads, hats)], axis=0
        ).astype(BF)
        dy = dot(perm_ref[...], back, TN).astype(BF)

        s_dy[rows, :] = dy
        dhidden = dot(dy, wdown_ref[...], NT).astype(BF).astype(F32)
        du = (dhidden * slope).astype(BF)
        s_du[rows, :] = du
        dn = dot(du, wup_ref[...], NT).astype(BF).astype(F32) * g2_ref[...]
        da = (dy.astype(F32) + norm_grad(hat2, scale2, dn)).astype(BF)
        s_da[rows, :] = da

        dmixed[...] = dot(da, wproj_ref[...], NT).astype(BF)
        for h in range(HEADS):
            q = triple[0:WIN, h * HEAD:(h + 1) * HEAD]
            k = triple[:, C + h * HEAD:C + (h + 1) * HEAD]
            v = triple[:, 2 * C + h * HEAD:2 * C + (h + 1) * HEAD]
            dm = dmixed[:, h * HEAD:(h + 1) * HEAD]
            p = prob[h]
            dp = dot(dm, v, NT).astype(BF).astype(F32)
            ds = p * (dp - jnp.sum(dp * p, axis=-1, keepdims=True))
            where_rows = pl.ds(t * HEADS + h, WIN, stride=TH)
            dscore[0, where_rows, :] = ds[:, :LANES]
            dscore[1, where_rows, :] = ds[:, LANES:]
            dsb = (ds * root).astype(BF)
            dtriple[:, h * HEAD:(h + 1) * HEAD] = dot(dsb, k).astype(BF)
            dtriple[:, C + h * HEAD:C + (h + 1) * HEAD] = dot(dsb, q, TN)[:WIN].astype(BF)
            dtriple[:, 2 * C + h * HEAD:2 * C + (h + 1) * HEAD] = dot(
                p.astype(BF), dm, TN
            )[:WIN].astype(BF)
        dt = dtriple[...]
        s_dtriple[rows, :] = dt
        dn1 = dot(dt, wqkv_ref[...], NT).astype(BF).astype(F32) * g1_ref[...]
        fgrad_ref[rows, :] = (da.astype(F32) + norm_grad(hat1, scale1, dn1)).astype(BF)
        return carry

    lax.fori_loop(0, TYPES, one_type, 0)

    def pack(first_block, value):
        for b in range(value.shape[1] // LANES):
            start = (first_block + b) * C
            packed_ref[start:start + C, :] = value[:, b * LANES:(b + 1) * LANES].astype(BF)

    pack(0, jnp.concatenate(
        [dot(s_normed[...], s_dtriple[...], TN), dot(s_mixed[...], s_da[...], TN)], axis=1))
    pack(6, dot(s_nmlp[...], s_du[...], TN))
    down = dot(s_hidden[...], s_dy[...], TN)
    pack(12, jnp.concatenate([down[g * C:(g + 1) * C] for g in range(4)], axis=1))
    for g in range(4):
        pack(18 + 3 * g, s_merge[g * C:(g + 1) * C, :])

    s_table[...] = jnp.zeros_like(s_table)

    def some_rows(step, carry):
        hots, lefts = [], []
        for u in range(UNROLL):
            i = step * UNROLL + u
            lane = lane_ref[pl.ds(i, 1), :]
            digit = digit_ref[pl.ds(i, 1), :]
            hots.append((lax.broadcasted_iota(jnp.int32, (RADIX, KEYS), 0) == lane).astype(BF))
            rows = pl.ds(pl.multiple_of(i * TH, TH), TH)
            ds = jnp.concatenate([dscore[0, rows, :], dscore[1, rows, :]], axis=1)
            lefts.append(jnp.concatenate(
                [jnp.where(digit == d, ds, 0.0) for d in range(DIGITS)], axis=0
            ).astype(BF))
        s_table[...] += dot(
            jnp.concatenate(lefts, axis=1), jnp.concatenate(hots, axis=1), NT
        )
        return carry

    lax.fori_loop(0, WIN // UNROLL, some_rows, 0)
    for b in range(2):
        start = ROWS_W + b * DIGITS * TH
        packed_ref[start:start + DIGITS * TH, :] = s_table[:, b * LANES:(b + 1) * LANES].astype(BF)
    end = ROWS_W + ROWS_T
    if packed_ref.shape[0] > end:
        packed_ref[end:, :] = jnp.zeros((packed_ref.shape[0] - end, LANES), BF)


def reduce_kernel(
    n, share, factor, packed_ref,
    qkv_ref, proj_ref, up_ref, down_ref, merge_ref, table_ref,
    paired, pair_sum, arrived, gathered,
    send0, recv0, send1, recv1, send2, recv2, send3, recv3,
):
    chips = n // 2
    me = lax.axis_index("lon")
    chip, core = me // 2, lax.rem(me, 2)
    partner = 2 * chip + 1 - core

    def across(k):
        return 2 * lax.rem(chip + k, chips) + core

    def rows_of(half, index):
        return pl.ds(pl.multiple_of((half * chips + index) * share, 16), share)

    def sent(src, dst, send, recv, device):
        copy = pltpu.make_async_remote_copy(
            src_ref=src, dst_ref=dst, send_sem=send, recv_sem=recv,
            device_id={"lon": device}, device_id_type=pl.DeviceIdType.MESH,
        )
        copy.start()
        return copy

    barrier = pltpu.get_barrier_semaphore()
    for device in [partner] + [across(k) for k in range(1, chips)]:
        pl.semaphore_signal(
            barrier, inc=1, device_id={"lon": device}, device_id_type=pl.DeviceIdType.MESH
        )
    pl.semaphore_wait(barrier, chips)

    order = list(range(1, chips)) + [0]
    stage0 = {}
    for k in order:
        stage0[k] = sent(
            packed_ref.at[rows_of(1 - core, lax.rem(chip + k, chips)), :],
            paired.at[k], send0.at[k], recv0.at[k], partner,
        )
    stage1 = {}
    total = None
    for k in order:
        stage0[k].wait_recv()
        own = packed_ref[rows_of(core, lax.rem(chip + k, chips)), :].astype(F32)
        summed = own + paired[k].astype(F32)
        if k == 0:
            total = summed
        else:
            pair_sum[k] = summed.astype(BF)
            stage1[k] = sent(
                pair_sum.at[k], arrived.at[k], send1.at[k], recv1.at[k], across(k)
            )
    for k in range(1, chips):
        stage1[k].wait_recv()
        total = total + arrived[k].astype(F32)
    mine = rows_of(core, chip)
    gathered[mine, :] = total.astype(BF)
    stage2 = {}
    for k in range(1, chips):
        stage2[k] = sent(
            gathered.at[mine, :], gathered.at[mine, :], send2.at[k], recv2.at[k], across(k)
        )
    stage3 = [sent(
        gathered.at[mine, :], gathered.at[mine, :], send3.at[0], recv3.at[0], partner
    )]
    for k in range(1, chips):
        stage2[k].wait_recv()
        rows = rows_of(core, lax.rem(chip - k + chips, chips))
        stage3.append(sent(
            gathered.at[rows, :], gathered.at[rows, :], send3.at[k], recv3.at[k], partner
        ))
    for k in order:
        stage0[k].wait_send()
    for k in range(1, chips):
        stage1[k].wait_send()
        stage2[k].wait_send()
    for copy in stage3:
        copy.wait()

    def block(index):
        return gathered[index * C:(index + 1) * C, :].astype(F32) * factor

    def joined(start, count):
        return jnp.concatenate([block(start + b) for b in range(count)], axis=1)

    front = joined(0, 6)
    qkv_ref[...] = front[:, :3 * C]
    proj_ref[...] = front[:, 3 * C:]
    up_ref[...] = joined(6, 6)
    downs = joined(12, 6)
    for g in range(4):
        down_ref[g * C:(g + 1) * C, :] = downs[:, g * C:(g + 1) * C]
        merge_ref[g * C:(g + 1) * C, :] = joined(18 + 3 * g, 3)
    for b in range(2):
        start = ROWS_W + b * DIGITS * TH
        half = gathered[start:start + DIGITS * TH, :].astype(F32) * factor
        for d in range(DIGITS):
            at = d * RADIX + b * LANES
            table_ref[:, at:at + LANES] = half[d * TH:(d + 1) * TH]


def passed_along(value, axis, steps):
    count = lax.axis_size(axis)
    return lax.ppermute(value, axis, [(s, (s + steps) % count) for s in range(count)])


def group_order():
    order = np.zeros((4 * GPAD, WIN), np.float32)
    for pa in range(2):
        for pb in range(2):
            for z in range(WZ):
                for a in range(WLAT // 2):
                    for b in range(WLON // 2):
                        cell = (z * (WLAT // 2) + a) * (WLON // 2) + b
                        token = (z * WLAT + 2 * a + pa) * WLON + 2 * b + pb
                        order[(2 * pa + pb) * GPAD + cell, token] = 1.0
    return jnp.asarray(order, BF)


def local(
    fields, norm_gain, qkv_weight, proj_weight, bias_table, bias_index, region_ids,
    mlp_gain, up_weight, down_weight, merge_gain, merge_weight, cotangent,
):
    n = lax.axis_size("lon")
    windows = fields.shape[2] // WLON
    assert windows == 1
    bands = LAT // WLAT
    west_fields = passed_along(fields[:, :, :HALF], "lon", -1)
    west_ct = passed_along(cotangent[:, :, :HALF // 2], "lon", -1)

    table = jnp.pad(bias_table.reshape(TH, BPOS), ((0, 0), (0, DIGITS * RADIX - BPOS)))
    table = table.reshape(TH, DIGITS, RADIX).transpose(1, 0, 2).reshape(DIGITS * TH, RADIX)
    table = table.astype(BF)
    index = jnp.pad(bias_index, ((0, 0), (0, KEYS - WIN)), constant_values=-1)
    digit = index >> 8
    lane = jnp.where(index < 0, -1, index & (RADIX - 1))
    bias = pl.pallas_call(
        bias_kernel,
        out_shape=jax.ShapeDtypeStruct((2, WIN * TH, LANES), F32),
        in_specs=[VMEM] * 3,
        out_specs=VMEM,
        compiler_params=pltpu.CompilerParams(vmem_limit_bytes=24 << 20),
        cost_estimate=pl.CostEstimate(flops=7_000_000_000, bytes_accessed=4 << 20, transcendentals=0),
        name="bias_rows",
    )(table, digit, lane)

    labels = region_ids.reshape(WZ, bands, WLAT).transpose(1, 0, 2).reshape(TYPES, WZ * WLAT)
    labels = jnp.repeat(labels, WLON, axis=1)
    label_keys = jnp.pad(labels, ((0, 0), (0, KEYS - WIN)), constant_values=-1)

    shifted = jnp.concatenate([fields[:, :, HALF:], west_fields], axis=2)
    tokens = shifted.reshape(WZ, bands, WLAT, WLON, C).transpose(1, 0, 2, 3, 4).reshape(TYPES * WIN, C)
    ct = jnp.concatenate([cotangent[:, :, HALF // 2:], west_ct], axis=2)
    ct = ct.reshape(WZ, bands, WLAT // 2, WLON // 2, 2 * C).transpose(1, 0, 2, 3, 4)
    ct = jnp.pad(ct.reshape(TYPES, GROUP, 2 * C), ((0, 0), (0, GPAD - GROUP), (0, 0)))

    share = -(-(ROWS_W + ROWS_T) // (16 * n)) * 16
    total_rows = TYPES * WIN
    merged_win, fgrad_win, packed = pl.pallas_call(
        block_kernel,
        out_shape=(
            jax.ShapeDtypeStruct((TYPES, GPAD, 2 * C), BF),
            jax.ShapeDtypeStruct((total_rows, C), BF),
            jax.ShapeDtypeStruct((n * share, LANES), BF),
        ),
        in_specs=[VMEM] * 16,
        out_specs=(VMEM,) * 3,
        scratch_shapes=[
            pltpu.VMEM((KEYS, 3 * C), BF),
            pltpu.VMEM((HEADS, WIN, KEYS), F32),
            pltpu.VMEM((WIN, C), BF),
            pltpu.VMEM((WIN, C), BF),
            pltpu.VMEM((WIN, 3 * C), BF),
            pltpu.VMEM((2, WIN * TH, LANES), F32),
            pltpu.VMEM((total_rows, C), BF),
            pltpu.VMEM((total_rows, 3 * C), BF),
            pltpu.VMEM((total_rows, C), BF),
            pltpu.VMEM((total_rows, C), BF),
            pltpu.VMEM((total_rows, C), BF),
            pltpu.VMEM((total_rows, MLP), BF),
            pltpu.VMEM((total_rows, MLP), BF),
            pltpu.VMEM((total_rows, C), BF),
            pltpu.VMEM((4 * C, 2 * C), F32),
            pltpu.VMEM((DIGITS * TH, RADIX), F32),
        ],
        compiler_params=pltpu.CompilerParams(vmem_limit_bytes=48 << 20),
        cost_estimate=pl.CostEstimate(flops=20_000_000_000, bytes_accessed=8 << 20, transcendentals=2_000_000),
        name="block",
    )(
        tokens, ct, bias, labels[:, :, None], label_keys[:, None, :], digit, lane, group_order(),
        norm_gain[None], qkv_weight, proj_weight, mlp_gain[None], up_weight, down_weight,
        merge_gain.reshape(4, C), merge_weight,
    )

    merged_grid = merged_win[:, :GROUP].reshape(bands, WZ, WLAT // 2, WLON // 2, 2 * C)
    merged_grid = merged_grid.transpose(1, 0, 2, 3, 4).reshape(Z, LAT // 2, WLON // 2, 2 * C)
    fgrad_grid = fgrad_win.reshape(bands, WZ, WLAT, WLON, C)
    fgrad_grid = fgrad_grid.transpose(1, 0, 2, 3, 4).reshape(Z, LAT, WLON, C)
    east_merged = passed_along(merged_grid[:, :, HALF // 2:], "lon", 1)
    east_fgrad = passed_along(fgrad_grid[:, :, HALF:], "lon", 1)
    merged = jnp.concatenate([east_merged, merged_grid[:, :, :HALF // 2]], axis=2)
    field_grad = jnp.concatenate([east_fgrad, fgrad_grid[:, :, :HALF]], axis=2)

    factor = float(Z * LAT * fields.shape[2] * n) ** (-0.5)
    outs = pl.pallas_call(
        functools.partial(reduce_kernel, n, share, factor),
        out_shape=(
            jax.ShapeDtypeStruct((C, 3 * C), F32),
            jax.ShapeDtypeStruct((C, C), F32),
            jax.ShapeDtypeStruct((C, MLP), F32),
            jax.ShapeDtypeStruct((MLP, C), F32),
            jax.ShapeDtypeStruct((4 * C, 2 * C), F32),
            jax.ShapeDtypeStruct((TH, DIGITS * RADIX), F32),
        ),
        in_specs=[VMEM],
        out_specs=(VMEM,) * 6,
        scratch_shapes=[
            pltpu.VMEM((n // 2, share, LANES), BF),
            pltpu.VMEM((n // 2, share, LANES), BF),
            pltpu.VMEM((n // 2, share, LANES), BF),
            pltpu.VMEM((n * share, LANES), BF),
        ] + [pltpu.SemaphoreType.DMA((n // 2,))] * 8,
        compiler_params=pltpu.CompilerParams(
            collective_id=0, has_side_effects=True, vmem_limit_bytes=24 << 20
        ),
        cost_estimate=pl.CostEstimate(flops=10_000_000_000, bytes_accessed=16 << 20, transcendentals=0),
        name="weight_sums",
    )(packed)
    qkv_grad, proj_grad, up_grad, down_grad, merge_grad, table_grad = outs
    table_grad = table_grad[:, :BPOS].reshape(TYPES, HEADS, BPOS)
    return (
        merged, field_grad, qkv_grad, proj_grad, up_grad, down_grad, merge_grad, table_grad,
    )


def solution(mesh):
    grid = P("groups", None, "lon", None)
    rows = P("groups", None)
    return jax.shard_map(
        local,
        mesh=mesh,
        in_specs=(grid,) + (P(),) * 11 + (grid,),
        out_specs=(grid, grid) + (rows,) * 5 + (P("groups", None, None),),
        check_vma=False,
    )
```

profile of v0, /device:TPU:27, one launch (start us, length us, event | category | flops | bytes accessed | tf_op | source)
XLA Modules:
  0.0 132.6 jit_solution(4272041722288261952)
XLA Ops:
  0.6 1.0 fusion.3
  1.6 0.7 collective-permute-start.1
  2.3 1.0 fusion.1
  3.4 1.0 convert.5
  4.9 12.2 %bias_rows.1.bias_ref = f32[2,3456,128]{2,1,0:T(8,128)S(1)} custom-call(bf16[312,256]{1,0:T(8,128)(2,1)S(1)} %bitcast.20, s32[144,256]{1,0:T(8,128)S(1)} %get-tuple-element.55.digit_ref, s32[144,256]{1,0:T(8,128)S(1)} %get-tuple-element.54.lane_ref), custom_call_target="tpu_custom_call" | custom-call | flops 7000000000 | bytes 4194304 | tf_op jit(solution)/shard_map/bias_rows/pallas_call | solution.py:364
  17.1 1.7 %copy-done.9 = f32[2,3456,128]{2,1,0:T(8,128)} copy-done((f32[2,3456,128]{2,1,0:T(8,128)}, f32[2,3456,128]{2,1,0:T(8,128)S(1)}, u32[]{:S(2)}) %copy-start.9) | copy-done | bytes 3538968
  21.0 44.5 %block.1 = (bf16[4,48,384]{2,1,0:T(8,128)(2,1)S(1)}, bf16[576,192]{1,0:T(8,128)(2,1)S(1)}, bf16[6400,128]{1,0:T(8,128)(2,1)S(1)}) custom-call(bf16[576,192]{1,0:T(8,128)(2,1)S(1)} %reshape.64.x_ref, bf16[4,48,384]{2,1,0:T(8,128)(2,1)S(1)} %pad.17.ct_ref, f32[2,3456,128]{2,1,0:T(8,128)} %copy-done.9, s32[4,144,1]{2,1,0:T(8,128)S(1)} %broadcast_in_dim_reshape.4.regq_ref, ...), custom_call_target="tpu_custom_call" | custom-call | flops 20000000000 | bytes 8388608 | tf_op jit(solution)/shard_map/block/pallas_call | solution.py:386
  65.5 1.2 copy-done.10
  66.9 0.7 fusion.2
  67.6 4.4 %collective-permute-start.2 = (bf16[2,12,3,384]{3,0,2,1:T(2,128)(2,1)}, bf16[2,12,3,384]{3,0,2,1:T(2,128)(2,1)}, u32[]{:S(2)}, u32[]{:S(2)}) collective-permute-start(bf16[2,12,3,384]{3,0,2,1:T(2,128)(2,1)} %get-tuple-element.56), channel_id=1, source_target_pairs={{0,1},{1,2},{2,3},{3,4},{4,5},{5,6},{6,7},{7,8},{8,9},{9,10},{10,1... | collective-permute-start | bytes 165896 | tf_op jit(solution)/shard_map/ppermute | solution.py:331
  72.5 0.9 fusion
  73.3 1.4 %copy-done.11 = bf16[6400,128]{1,0:T(8,128)(2,1)S(1)} copy-done((bf16[6400,128]{1,0:T(8,128)(2,1)S(1)}, bf16[6400,128]{1,0:T(8,128)(2,1)}, u32[]{:S(2)}) %copy-start.11) | copy-done | bytes 1638424
  74.8 46.4 %weight_sums.1 = (f32[192,576]{1,0:T(8,128)S(1)}, f32[192,192]{1,0:T(8,128)S(1)}, f32[192,768]{1,0:T(8,128)S(1)}, f32[768,192]{1,0:T(8,128)S(1)}, f32[768,384]{1,0:T(8,128)S(1)}, /*index=5*/f32[24,3328]{1,0:T(8,128)S(1)}) custom-call(bf16[6400,128]{1,0:T(8,128)(2,1)S(1)} %copy-done.11), custom_call_target="tpu_custom_call" | custom-call | flops 10000000000 | bytes 16777216 | tf_op jit(solution)/shard_map/weight_sums/pallas_call | solution.py:432
  121.2 0.7 copy-done
  121.9 0.8 reshape.76
  122.7 1.9 %copy.58 = f32[4,6,3312]{2,0,1:T(4,128)} copy(f32[4,6,3312]{2,1,0:T(8,128)} %reshape.76) | data formatting | bytes 635904
  124.5 1.1 copy.57
  125.6 1.6 %pad_maximum_fusion.3 = bf16[2,12,6,384]{3,0,2,1:T(2,128)(2,1)} fusion(bf16[2,12,3,384]{3,0,2,1:T(2,128)(2,1)S(1)} %copy-done.13, bf16[2,12,3,384]{3,0,2,1:T(2,128)(2,1)} %collective-permute-done.2), kind=kLoop, calls=%fused_computation.5 | loop fusion | flops 55296 | bytes 221184 | tf_op jit(solution)/shard_map/concatenate | solution.py:428
  127.2 1.3 %pad_maximum_fusion.1 = bf16[2,24,12,192]{3,0,2,1:T(2,128)(2,1)S(1)} fusion(bf16[2,24,6,192]{3,0,2,1:T(2,128)(2,1)S(1)} %get-tuple-element.51, bf16[2,24,6,192]{3,0,2,1:T(2,128)(2,1)} %collective-permute-done.3), kind=kLoop, calls=%fused_computation.1 | loop fusion | flops 110592 | bytes 442368 | tf_op jit(solution)/shard_map/concatenate | solution.py:429
  128.6 0.8 copy.56
  129.3 0.8 copy.63
  130.1 0.7 copy.64
  130.8 0.8 copy.65
  131.6 1.0 copy.66
  (65 shorter events, 3.1 us)
Async XLA Ops:
  0.6 4.2 %copy-start.14 = (s32[144,144]{1,0:T(8,128)S(1)}, s32[144,144]{1,0:T(8,128)}, u32[]{:S(2)}) copy-start(s32[144,144]{1,0:T(8,128)} %param.19) | copy-start | bytes 248836
  1.6 18.0 %collective-permute-start.1 = (bf16[2,12,3,384]{3,0,2,1:T(2,128)(2,1)S(1)}, bf16[2,12,3,384]{3,0,2,1:T(2,128)(2,1)S(1)}, u32[]{:S(2)}, u32[]{:S(2)}) collective-permute-start(bf16[2,12,3,384]{3,0,2,1:T(2,128)(2,1)S(1)} %get-tuple-element.59), channel_id=1, source_target_pairs={{0,15},{1,0},{2,1},{3,2},{4,3},{5,4},{6,5},{7,6},{8,7},{9,8},{10,9... | collective-permute-start | bytes 165896 | tf_op jit(solution)/shard_map/ppermute | solution.py:331
  3.3 16.6 %collective-permute-start = (bf16[2,24,6,192]{3,1,2,0:T(8,128)(2,1)S(1)}, bf16[2,24,6,192]{3,1,2,0:T(8,128)(2,1)S(1)}, u32[]{:S(2)}, u32[]{:S(2)}) collective-permute-start(bf16[2,24,6,192]{3,1,2,0:T(8,128)(2,1)S(1)} %get-tuple-element.53), channel_id=1, source_target_pairs={{0,15},{1,0},{2,1},{3,2},{4,3},{5,4},{6,5},{7,6},{8,7},{9,8},{10,9... | collective-permute-start | bytes 331784 | tf_op jit(solution)/shard_map/ppermute | solution.py:331
  4.8 13.9 %copy-start.16 = (s32[2,24]{1,0:T(2,128)S(1)}, s32[2,24]{1,0:T(2,128)}, u32[]{:S(2)}) copy-start(s32[2,24]{1,0:T(2,128)} %param.20) | copy-start | bytes 580
  4.9 14.4 %copy-start.15 = (f32[768]{0:T(1024)S(1)}, f32[768]{0:T(1024)}, u32[]{:S(2)}) copy-start(f32[768]{0:T(1024)} %param.24) | copy-start | bytes 9220
  4.9 14.5 %copy-start.12 = (bf16[768,192]{0,1:T(8,128)(2,1)S(1)}, bf16[768,192]{0,1:T(8,128)(2,1)}, u32[]{:S(2)}) copy-start(bf16[768,192]{0,1:T(8,128)(2,1)} %param.23) | copy-start | bytes 884740
  17.1 1.7 %copy-start.9 = (f32[2,3456,128]{2,1,0:T(8,128)}, f32[2,3456,128]{2,1,0:T(8,128)S(1)}, u32[]{:S(2)}) copy-start(f32[2,3456,128]{2,1,0:T(8,128)S(1)} %bias_rows.1.bias_ref) | copy-start | bytes 10616836
  19.7 1.1 copy-start.2
  19.8 1.1 copy-start.3
  19.8 1.2 copy-start.4
  19.8 1.2 copy-start.5
  19.8 1.2 copy-start.6
  19.8 1.2 copy-start.7
  19.8 1.2 copy-start.8
  65.5 1.2 copy-start.10
  67.6 58.0 %collective-permute-start.2 = (bf16[2,12,3,384]{3,0,2,1:T(2,128)(2,1)}, bf16[2,12,3,384]{3,0,2,1:T(2,128)(2,1)}, u32[]{:S(2)}, u32[]{:S(2)}) collective-permute-start(bf16[2,12,3,384]{3,0,2,1:T(2,128)(2,1)} %get-tuple-element.56), channel_id=1, source_target_pairs={{0,1},{1,2},{2,3},{3,4},{4,5},{5,6},{6,7},{7,8},{8,9},{9,10},{10,1... | collective-permute-start | bytes 165896 | tf_op jit(solution)/shard_map/ppermute | solution.py:331
  73.3 53.9 %collective-permute-start.3 = (bf16[2,24,6,192]{3,0,2,1:T(2,128)(2,1)}, bf16[2,24,6,192]{3,0,2,1:T(2,128)(2,1)}, u32[]{:S(2)}, u32[]{:S(2)}) collective-permute-start(bf16[2,24,6,192]{3,0,2,1:T(2,128)(2,1)} %get-tuple-element.50), channel_id=1, source_target_pairs={{0,1},{1,2},{2,3},{3,4},{4,5},{5,6},{6,7},{7,8},{8,9},{9,10},{10,1... | collective-permute-start | bytes 331784 | tf_op jit(solution)/shard_map/ppermute | solution.py:331
  73.3 1.4 %copy-start.11 = (bf16[6400,128]{1,0:T(8,128)(2,1)S(1)}, bf16[6400,128]{1,0:T(8,128)(2,1)}, u32[]{:S(2)}) copy-start(bf16[6400,128]{1,0:T(8,128)(2,1)} %copy-done.10) | copy-start | bytes 4915204
  121.2 0.7 copy-start
  122.7 2.9 %copy-start.13 = (bf16[2,12,3,384]{3,0,2,1:T(2,128)(2,1)S(1)}, bf16[2,12,3,384]{3,0,2,1:T(2,128)(2,1)}, u32[]{:S(2)}) copy-start(bf16[2,12,3,384]{3,0,2,1:T(2,128)(2,1)} %get-tuple-element.57) | copy-start | bytes 165892
  124.5 5.6 %copy-start.1 = (f32[192,192]{1,0:T(8,128)S(1)}, f32[192,192]{1,0:T(8,128)}, u32[]{:S(2)}) copy-start(f32[192,192]{1,0:T(8,128)} %copy-done) | copy-start | bytes 442372
where the time goes:
time: 133 us
  Pallas kernels  103 us (77%)
  local copies, waits for them, and re-layouts  19.1 us (14%)
  starting transfers between devices  5.23 us (4%)
  other arithmetic  4.2 us (3%)
    pallas_call x1, Pallas kernels, local(): pl.pallas_call(functools.partial(reduce_kernel, n, share, factor), out_sh...  46.4 us
    pallas_call x1, Pallas kernels, local(): pl.pallas_call(block_kernel, out_shape=(jax.ShapeDtypeStruct((TYPES, GPAD...  44.5 us
    unnamed x42, local copies, waits for them, and re-layouts  12.8 us
    pallas_call x1, Pallas kernels, local(): pl.pallas_call(bias_kernel, out_shape=jax.ShapeDtypeStruct((2, WIN * TH,...  12.2 us
    ppermute x4, starting transfers between devices, passed_along(): lax.ppermute(value, axis, [(s, (s + steps) % count) for s in range(count)])  5.23 us
  transfers between devices with their start and end apart: 4, of which 0 were waited for; matrix products, arithmetic and copies ran while one was open for 7% of the time, Pallas kernels for 44%

commit v1 on v0

v1 whole, which is shorter than its diff:
```python
import functools

import jax
import jax.numpy as jnp
import numpy as np
from jax import lax
from jax.experimental import pallas as pl
from jax.experimental.pallas import tpu as pltpu
from jax.sharding import PartitionSpec as P

C = 192
MLP = 768
HEADS = 6
HEAD = 32
WZ = 2
WLAT = 6
WLON = 12
HALF = 6
WIN = 144
BPOS = 3312
Z = 2
LAT = 24
TYPES = 4
TH = TYPES * HEADS
LANES = 128
RADIX = 256
DIGITS = -(-BPOS // RADIX)
GROUP = WIN // 4
GPAD = 48
TAIL = WIN - LANES
WIDE = (HEADS + 1) * LANES
TOK = TYPES * WIN
UNROLL = 4
ROWS = (18 * LANES, 12 * C, 6 * C, 2 * DIGITS * TH)
BF = jnp.bfloat16
F32 = jnp.float32
VMEM = pl.BlockSpec(memory_space=pltpu.VMEM)
ANY = pl.BlockSpec(memory_space=pl.ANY)
NT = ((1,), (1,))
TN = ((0,), (0,))


def dot(a, b, dims=((1,), (0,))):
    return lax.dot_general(a, b, (dims, ((), ())), preferred_element_type=F32)


def norm_parts(values):
    average = jnp.mean(values, axis=-1, keepdims=True)
    centred = values - average
    variance = jnp.mean(centred * centred, axis=-1, keepdims=True)
    scale = lax.rsqrt(variance + 1e-05)
    return centred * scale, scale


def norm_grad(hat, scale, grad_hat):
    first = jnp.mean(grad_hat, axis=-1, keepdims=True)
    second = jnp.mean(grad_hat * hat, axis=-1, keepdims=True)
    return scale * (grad_hat - first - hat * second)


def grid_sides(n):
    chips = n // 2
    fast = 1
    while fast * fast * 8 <= chips:
        fast *= 2
    return chips // fast, fast


def piece_rows(n):
    step = 16 * n
    return [-(-rows // step) * step for rows in ROWS]


class Sum:
    def __init__(self, n, rows, packed, out, paired, half_sum, crossed, part_sum, landed, send, recv):
        self.slow, self.fast = grid_sides(n)
        self.share = rows // n
        me = lax.axis_index("lon")
        self.core = lax.rem(me, 2)
        self.x = lax.rem(me // 2, self.fast)
        self.z = me // (2 * self.fast)
        self.packed, self.out = packed, out
        self.paired, self.half_sum, self.crossed = paired, half_sum, crossed
        self.part_sum, self.landed = part_sum, landed
        self.send, self.recv = send, recv
        self.used = 0
        self.started = []

    def device(self, z, x, core):
        return (z * self.fast + x) * 2 + core

    def copy(self, src, dst, device):
        made = pltpu.make_async_remote_copy(
            src_ref=src, dst_ref=dst, send_sem=self.send.at[self.used],
            recv_sem=self.recv.at[self.used],
            device_id={"lon": device}, device_id_type=pl.DeviceIdType.MESH,
        )
        made.start()
        self.used += 1
        self.started.append(made)
        return made

    def at(self, index, count):
        return pl.ds(pl.multiple_of(index * self.share, 16), count * self.share)

    def across_x(self):
        return [lax.rem(self.x + k, self.fast) for k in range(1, self.fast)]

    def across_z(self):
        return [lax.rem(self.z + k, self.slow) for k in range(1, self.slow)]

    def s0(self):
        count = self.slow * self.fast
        other = 1 - self.core
        self.waits = [self.copy(
            self.packed.at[self.at(other * count, count), :], self.paired,
            self.device(self.z, self.x, other),
        )]

    def s1(self):
        count = self.slow * self.fast
        self.waits[0].wait_recv()
        mine = self.packed[self.at(self.core * count, count), :].astype(F32)
        self.half_sum[...] = (mine + self.paired[...].astype(F32)).astype(BF)
        self.waits = [
            self.copy(
                self.half_sum.at[self.at(x * self.slow, self.slow), :], self.crossed.at[k],
                self.device(self.z, x, self.core),
            )
            for k, x in enumerate(self.across_x())
        ]

    def s2(self):
        total = self.half_sum[self.at(self.x * self.slow, self.slow), :].astype(F32)
        for k, made in enumerate(self.waits):
            made.wait_recv()
            total = total + self.crossed[k].astype(F32)
        self.part_sum[...] = total.astype(BF)
        self.waits = [
            self.copy(
                self.part_sum.at[self.at(z, 1), :], self.landed.at[k],
                self.device(z, self.x, self.core),
            )
            for k, z in enumerate(self.across_z())
        ]

    def s3(self):
        total = self.part_sum[self.at(self.z, 1), :].astype(F32)
        for k, made in enumerate(self.waits):
            made.wait_recv()
            total = total + self.landed[k].astype(F32)
        rows = self.at((self.core * self.fast + self.x) * self.slow + self.z, 1)
        self.out[rows, :] = total.astype(BF)
        self.waits = [
            self.copy(
                self.out.at[rows, :], self.out.at[rows, :], self.device(z, self.x, self.core)
            )
            for z in self.across_z()
        ]

    def s4(self):
        for made in self.waits:
            made.wait_recv()
        rows = self.at((self.core * self.fast + self.x) * self.slow, self.slow)
        self.waits = [
            self.copy(
                self.out.at[rows, :], self.out.at[rows, :], self.device(self.z, x, self.core)
            )
            for x in self.across_x()
        ]

    def s5(self):
        for made in self.waits:
            made.wait_recv()
        count = self.slow * self.fast
        rows = self.at(self.core * count, count)
        self.waits = [self.copy(
            self.out.at[rows, :], self.out.at[rows, :], self.device(self.z, self.x, 1 - self.core)
        )]

    def s6(self):
        for made in self.waits:
            made.wait_recv()
        for made in self.started:
            made.wait_send()


def block_kernel(
    n,
    gains_ref, tail_index_ref, labels_ref, perm_ref,
    fields_hbm, ct_hbm, table_hbm, index_hbm, wqkv_hbm, wproj_hbm, wup_hbm, wdown_hbm, wm_hbm,
    merged_ref, fgrad_ref, out1, out2, out3, out4,
    fields, east, ct, east_ct, table, index, wqkv, wproj, wup, wdown, wm, in_sem,
    edge_send, edge_recv, merged_in, merged_out, fgrad_in, fgrad_out,
    packed1, packed2, packed3, packed4,
    paired1, paired2, paired3, paired4, half1, half2, half3, half4,
    crossed1, crossed2, crossed3, crossed4, part1, part2, part3, part4,
    landed1, landed2, landed3, landed4, send1, send2, send3, send4, recv1, recv2, recv3, recv4,
    index_main, rows_in, ct_rows, xs, cts, tab, wt, bias, tail0, tail1, tails, eye,
    kbd, vbd, vbd2, wide, prob, probb, dsb, dscore, dtail0, dtail1, dtails,
    triple_t, s_normed, s_mixed, s_after, s_nmlp, s_slope, s_hidden, s_dy, s_nm, s_ct, s_du,
    s_da, s_dm, s_dt, grad_rows, merged_rows, s_table,
):
    me = lax.axis_index("lon")
    east_of, west_of = lax.rem(me + 1, n), lax.rem(me + n - 1, n)
    rows_of = piece_rows(n)
    sums = [
        Sum(n, rows, *refs) for rows, *refs in zip(
            rows_of, (packed1, packed2, packed3, packed4), (out1, out2, out3, out4),
            (paired1, paired2, paired3, paired4), (half1, half2, half3, half4),
            (crossed1, crossed2, crossed3, crossed4), (part1, part2, part3, part4),
            (landed1, landed2, landed3, landed4), (send1, send2, send3, send4),
            (recv1, recv2, recv3, recv4),
        )
    ]
    first = sums[0]

    local_copies = []
    for k, (src, dst) in enumerate((
        (table_hbm, table), (index_hbm, index), (fields_hbm, fields), (wqkv_hbm, wqkv),
        (wproj_hbm, wproj), (wup_hbm, wup), (wdown_hbm, wdown), (wm_hbm, wm), (ct_hbm, ct),
    )):
        made = pltpu.make_async_copy(src, dst, in_sem.at[k])
        made.start()
        local_copies.append(made)

    peers = [first.device(first.z, first.x, 1 - first.core), west_of, east_of]
    peers += [first.device(first.z, x, first.core) for x in first.across_x()]
    peers += [first.device(z, first.x, first.core) for z in first.across_z()]
    barrier = pltpu.get_barrier_semaphore()
    for device in peers:
        pl.semaphore_signal(
            barrier, inc=1, device_id={"lon": device}, device_id_type=pl.DeviceIdType.MESH
        )
    pl.semaphore_wait(barrier, len(peers))

    def edge(k, src, dst, device):
        made = pltpu.make_async_remote_copy(
            src_ref=src, dst_ref=dst, send_sem=edge_send.at[k], recv_sem=edge_recv.at[k],
            device_id={"lon": device}, device_id_type=pl.DeviceIdType.MESH,
        )
        made.start()
        return made

    edges = [
        edge(0, fields_hbm.at[:, :, 0:8, :], east, west_of),
        edge(1, ct_hbm, east_ct, west_of),
    ]

    for ref in (tab, kbd, vbd, vbd2, cts, dtails, tails):
        ref[...] = jnp.zeros_like(ref)
    eye[...] = (
        lax.broadcasted_iota(jnp.int32, (C, C), 0) == lax.broadcasted_iota(jnp.int32, (C, C), 1)
    ).astype(BF)

    local_copies[0].wait()
    for d in range(DIGITS):
        width = min(RADIX, BPOS - d * RADIX)
        for t in range(TYPES):
            start = d * TH + t * HEADS
            tab[start:start + HEADS, :width] = table[t, :, d * RADIX:d * RADIX + width]
    local_copies[1].wait()
    index_main[...] = index[:, 0:LANES]

    def position_of(where):
        digit = where >> 8
        lane = jnp.where(where < 0, -1, where & (RADIX - 1))
        hot = (lax.broadcasted_iota(jnp.int32, (RADIX, RADIX), 0) == lane).astype(BF)
        return digit, hot

    def main_position(pair):
        return position_of(jnp.concatenate(
            [index_main[pl.ds(2 * pair, 1), :], index_main[pl.ds(2 * pair + 1, 1), :]], axis=1
        ))

    def tail_position(key):
        return position_of(tail_index_ref[pl.ds(key, 1), :])

    table_bf = tab[...].astype(BF)
    tab_bf = dsb
    tab_bf[0:DIGITS * TH, 0:RADIX] = table_bf

    def looked_up(digit, hot):
        found = dot(tab_bf[0:DIGITS * TH, 0:RADIX], hot)
        total = jnp.zeros((TH, RADIX), F32)
        for d in range(DIGITS):
            total = jnp.where(digit == d, found[d * TH:(d + 1) * TH], total)
        return total

    def th_rows(i):
        return pl.ds(pl.multiple_of(i * TH, 8), TH)

    def main_bias(step, carry):
        for u in range(UNROLL):
            pair = step * UNROLL + u
            total = looked_up(*main_position(pair))
            bias[th_rows(2 * pair), :] = total[:, :LANES]
            bias[th_rows(2 * pair + 1), :] = total[:, LANES:]
        return carry

    lax.fori_loop(0, WIN // 2 // UNROLL, main_bias, 0)

    def tail_bias(step, carry):
        for u in range(UNROLL):
            key = step * UNROLL + u
            total = looked_up(*tail_position(key))
            tail0[th_rows(key), :] = total[:, :LANES]
            tail1[th_rows(key), :] = total[:, LANES:]
        return carry

    lax.fori_loop(0, TAIL // UNROLL, tail_bias, 0)

    for made in local_copies[2:4]:
        made.wait()
    wt[...] = dot(wqkv[...], eye[...], TN).astype(BF)
    edges[0].wait_recv()
    for z in range(Z):
        for a in range(LAT):
            k = z * LAT + a
            base = (a // WLAT) * WIN + z * WLAT * WLON + (a % WLAT) * WLON
            rows_in[16 * k:16 * k + WLON, :] = fields[z, a].astype(F32)
            xs[base:base + HALF, :] = rows_in[16 * k + HALF:16 * k + WLON, :]
    for z in range(Z):
        for a in range(LAT):
            k = z * LAT + a
            base = (a // WLAT) * WIN + z * WLAT * WLON + (a % WLAT) * WLON
            rows_in[16 * k:16 * k + 8, :] = east[z, a].astype(F32)
            xs[base + HALF:base + WLON, :] = rows_in[16 * k:16 * k + HALF, :]
    for made in local_copies[4:]:
        made.wait()
    edges[1].wait_recv()
    for part, ref in enumerate((ct, east_ct)):
        for z in range(Z):
            for a in range(LAT // 2):
                k = z * (LAT // 2) + a
                t, b = a // (WLAT // 2), a % (WLAT // 2)
                base = t * GPAD + z * (GROUP // 2) + b * HALF + part * (HALF // 2)
                ct_rows[8 * k:8 * k + HALF, :] = ref[z, a].astype(F32)
                skip = (1 - part) * (HALF // 2)
                cts[base:base + HALF // 2, :] = ct_rows[8 * k + skip:8 * k + skip + HALF // 2, :]
    s_ct[...] = cts[...].astype(BF)

    root = float(HEAD) ** (-0.5)
    low = -1e30
    lanes = lax.broadcasted_iota(jnp.int32, (1, LANES), 1)
    segs = [(lanes >= h * TAIL) & (lanes < (h + 1) * TAIL) for h in range(HEADS)]
    g1, g2 = gains_ref[0:1, :], gains_ref[1:2, :]

    def head_cols(h):
        return slice(h * LANES, (h + 1) * LANES)

    def place(dst, value_t):
        for h in range(HEADS):
            own = slice(h * HEAD, (h + 1) * HEAD)
            dst[own, head_cols(h)] = value_t[own, 0:LANES]
            at = HEADS * LANES + h * TAIL
            dst[own, at:at + TAIL] = value_t[own, LANES:WIN]

    def forward(t, carry):
        rows = pl.ds(pl.multiple_of(t * WIN, 16), WIN)
        field = xs[rows, :]
        hat1, _ = norm_parts(field)
        normed = (hat1 * g1).astype(BF)
        s_normed[rows, :] = normed
        triple_t[t] = dot(wt[...], normed, NT).astype(BF)
        q = dot(normed, wqkv[:, 0:C]).astype(BF)
        v = dot(normed, wqkv[:, 2 * C:3 * C]).astype(BF)
        place(kbd, triple_t.at[t, C:2 * C])
        for h in range(HEADS):
            own = slice(h * HEAD, (h + 1) * HEAD)
            vbd2[head_cols(h), own] = v[0:LANES, own]
            at = HEADS * LANES + h * TAIL
            vbd2[at:at + TAIL, own] = v[LANES:WIN, own]
        wide[...] = dot(q, kbd[...])

        label_q = labels_ref[pl.ds(t, 1), :]
        label_k = labels_ref[pl.ds(TYPES + t, 1), :]
        ids = lax.broadcasted_iota(jnp.int32, (8, RADIX), 0)
        same = dot((ids == label_q).astype(BF), (ids == label_k).astype(BF), TN)[0:WIN] > 0.5
        same_main, same_tail = same[:, :LANES], same[:, LANES:]

        for h in range(HEADS):
            picked = pl.ds(t * HEADS + h, TAIL, stride=TH)
            tails[h * TAIL:(h + 1) * TAIL, 0:LANES] = tail0[picked, :]
            tails[h * TAIL:(h + 1) * TAIL, LANES:] = tail1[picked, :]
        tail_bias_t = jnp.transpose(tails[...])[0:WIN]
        s_tail = jnp.where(same_tail, wide[:, HEADS * LANES:] * root + tail_bias_t, low)
        top_tail = jnp.zeros((WIN, LANES), F32)
        for h in range(HEADS):
            picked = pl.ds(t * HEADS + h, WIN, stride=TH)
            s = jnp.where(same_main, wide[:, head_cols(h)] * root + bias[picked, :], low)
            top = jnp.max(jnp.maximum(s, jnp.where(segs[h], s_tail, low)), axis=-1, keepdims=True)
            prob[t, :, head_cols(h)] = jnp.exp(s - top)
            top_tail = jnp.where(segs[h], top, top_tail)
        e_tail = jnp.exp(s_tail - top_tail)
        over_tail = jnp.zeros((WIN, LANES), F32)
        for h in range(HEADS):
            e = prob[t, :, head_cols(h)]
            over = 1.0 / jnp.sum(e + jnp.where(segs[h], e_tail, 0.0), axis=-1, keepdims=True)
            p = e * over
            prob[t, :, head_cols(h)] = p
            probb[t, :, head_cols(h)] = p.astype(BF)
            over_tail = jnp.where(segs[h], over, over_tail)
        p_tail = e_tail * over_tail
        prob[t, :, HEADS * LANES:] = p_tail
        probb[t, :, HEADS * LANES:] = p_tail.astype(BF)

        mixed = dot(probb[t], vbd2[...]).astype(BF)
        s_mixed[rows, :] = mixed
        branch = dot(mixed, wproj[...]).astype(BF).astype(F32)
        after_bf = (field + branch).astype(BF)
        s_after[rows, :] = after_bf
        after = after_bf.astype(F32)
        hat2, _ = norm_parts(after)
        nmlp = (hat2 * g2).astype(BF)
        s_nmlp[rows, :] = nmlp
        up = dot(nmlp, wup[...])
        cdf = 0.5 * (1.0 + lax.erf(up * np.float32(np.sqrt(0.5))))
        s_slope[rows, :] = cdf + up * (jnp.exp(-0.5 * up * up) * np.float32(1 / np.sqrt(2 * np.pi)))
        hidden = (up * cdf).astype(BF)
        s_hidden[rows, :] = hidden
        after_mlp = (after + dot(hidden, wdown[...])).astype(BF)

        spread = dot(perm_ref[...], after_mlp)
        parts = [spread[g * GPAD:(g + 1) * GPAD] for g in range(4)]
        average = sum(jnp.sum(p, axis=-1, keepdims=True) for p in parts) / (4 * C)
        parts = [p - average for p in parts]
        variance = sum(jnp.sum(p * p, axis=-1, keepdims=True) for p in parts) / (4 * C)
        scale = lax.rsqrt(variance + 1e-05)
        hats = [p * scale for p in parts]
        few = pl.ds(pl.multiple_of(t * GPAD, 16), GPAD)
        ct_t = s_ct[few, :]
        merged = jnp.zeros((GPAD, 2 * C), F32)
        grads = []
        for g in range(4):
            gain = gains_ref[2 + g:3 + g, :]
            weight = wm[g * C:(g + 1) * C, :]
            nm = (hats[g] * gain).astype(BF)
            s_nm[g, few, :] = nm
            merged = merged + dot(nm, weight)
            grads.append(dot(ct_t, weight, NT).astype(BF).astype(F32) * gain)
        merged_rows[few, :] = merged
        first = sum(jnp.sum(g, axis=-1, keepdims=True) for g in grads) / (4 * C)
        second = sum(
            jnp.sum(g * hat, axis=-1, keepdims=True) for g, hat in zip(grads, hats)
        ) / (4 * C)
        back = jnp.concatenate(
            [scale * (g - first - hat * second) for g, hat in zip(grads, hats)], axis=0
        ).astype(BF)
        s_dy[rows, :] = dot(perm_ref[...], back, TN).astype(BF)
        return carry

    lax.fori_loop(0, TYPES, forward, 0)

    def finish(packed, used):
        if packed.shape[0] > used:
            packed[used:, :] = jnp.zeros((packed.shape[0] - used, LANES), BF)

    for g in range(4):
        value = dot(s_nm[g], s_ct[...], TN)
        for b in range(3):
            packed1[b * 4 * C + g * C:b * 4 * C + (g + 1) * C, :] = (
                value[:, b * LANES:(b + 1) * LANES].astype(BF)
            )
    finish(packed1, ROWS[0])
    sums[0].s0()

    for z in range(Z):
        for a in range(LAT // 2):
            k = z * (LAT // 2) + a
            t, b = a // (WLAT // 2), a % (WLAT // 2)
            base = t * GPAD + z * (GROUP // 2) + b * HALF
            near, far = merged_rows[base:base + 3, :], merged_rows[base + 3:base + 6, :]
            ct_rows[8 * k + 3:8 * k + 6, :] = near
            cts[3 * k:3 * k + 3, :] = far
    merged_out[...] = cts[0:Z * LAT // 2 * 3, :].astype(BF)
    edges.append(edge(2, merged_out, merged_in, east_of))

    down = dot(s_hidden[...], s_dy[...], TN)
    packed2[0:MLP, :] = down[:, 0:LANES].astype(BF)
    packed2[MLP:MLP + MLP // 2, :] = jnp.concatenate(
        [down[0:MLP // 2, LANES:], down[MLP // 2:, LANES:]], axis=1
    ).astype(BF)
    sums[0].s1()

    def backward(t, carry):
        rows = pl.ds(pl.multiple_of(t * WIN, 16), WIN)
        dy = s_dy[rows, :]
        dhidden = dot(dy, wdown[...], NT).astype(BF).astype(F32)
        du = (dhidden * s_slope[rows, :]).astype(BF)
        s_du[rows, :] = du
        dn = dot(du, wup[...], NT).astype(BF).astype(F32) * g2
        hat2, scale2 = norm_parts(s_after[rows, :].astype(F32))
        da = (dy.astype(F32) + norm_grad(hat2, scale2, dn)).astype(BF)
        s_da[rows, :] = da
        return carry

    lax.fori_loop(0, TYPES, backward, 0)
    for b in range(6):
        value = dot(s_nmlp[...], s_du[:, b * LANES:(b + 1) * LANES], TN)
        start = 6 * C + b * C
        packed2[start:start + C, :] = value.astype(BF)
    finish(packed2, ROWS[1])
    sums[0].s2()
    sums[1].s0()

    def attend_back(t, carry):
        rows = pl.ds(pl.multiple_of(t * WIN, 16), WIN)
        da = s_da[rows, :]
        dm = dot(da, wproj[...], NT).astype(BF)
        dm_t = dot(wproj[...], da, NT).astype(BF)
        place(kbd, triple_t.at[t, C:2 * C])
        place(vbd, triple_t.at[t, 2 * C:3 * C])
        wide[...] = dot(dm, vbd[...]).astype(BF).astype(F32)
        dp_tail = wide[:, HEADS * LANES:]
        p_tail = prob[t, :, HEADS * LANES:]
        both_tail = dp_tail * p_tail
        sub_tail = jnp.zeros((WIN, LANES), F32)
        for h in range(HEADS):
            dp = wide[:, head_cols(h)]
            p = prob[t, :, head_cols(h)]
            sub = jnp.sum(dp * p + jnp.where(segs[h], both_tail, 0.0), axis=-1, keepdims=True)
            ds = p * (dp - sub)
            dscore[pl.ds(t * HEADS + h, WIN, stride=TH), :] = ds
            dsb[0:WIN, head_cols(h)] = (ds * root).astype(BF)
            sub_tail = jnp.where(segs[h], sub, sub_tail)
        ds_tail = p_tail * (dp_tail - sub_tail)
        dsb[0:WIN, HEADS * LANES:] = (ds_tail * root).astype(BF)
        dtails[0:WIN, :] = ds_tail
        turned = jnp.transpose(dtails[...])
        for h in range(HEADS):
            picked = pl.ds(t * HEADS + h, TAIL, stride=TH)
            dtail0[picked, :] = turned[h * TAIL:(h + 1) * TAIL, 0:LANES]
            dtail1[picked, :] = turned[h * TAIL:(h + 1) * TAIL, LANES:]

        s_dt[t, 0:C, :] = dot(kbd[...], dsb[0:WIN, :], NT).astype(BF)
        for part, (left, right) in enumerate((
            (triple_t[t, 0:C], dsb[0:WIN, :]), (dm_t, probb[t])
        )):
            base = (1 + part) * C
            over_tail = dot(left, right[:, HEADS * LANES:]).astype(BF)
            for h in range(HEADS):
                own = slice(h * HEAD, (h + 1) * HEAD)
                to = slice(base + h * HEAD, base + (h + 1) * HEAD)
                s_dt[t, to, 0:LANES] = dot(left[own], right[:, head_cols(h)]).astype(BF)
                s_dt[t, to, LANES:WIN] = over_tail[own, h * TAIL:(h + 1) * TAIL]
        dn1_t = dot(wqkv[...], s_dt[t]).astype(BF)
        dn1 = dot(dn1_t, eye[...], TN) * g1
        hat1, scale1 = norm_parts(xs[rows, :])
        grad_rows[rows, :] = da.astype(F32) + norm_grad(hat1, scale1, dn1)
        return carry

    lax.fori_loop(0, 2, attend_back, 0)
    sums[0].s3()
    sums[1].s1()
    lax.fori_loop(2, 3, attend_back, 0)
    sums[0].s4()
    sums[1].s2()
    lax.fori_loop(3, TYPES, attend_back, 0)

    total = dot(s_dt[0], s_normed[0:WIN, :])
    for t in range(1, TYPES):
        total = total + dot(s_dt[t], s_normed[t * WIN:(t + 1) * WIN, :])
    total = total.astype(BF)
    front = jnp.concatenate(
        [dot(total[k * C:(k + 1) * C], eye[...], TN) for k in range(3)]
        + [dot(s_mixed[...], s_da[...], TN)], axis=1,
    )
    for b in range(6):
        packed3[b * C:(b + 1) * C, :] = front[:, b * LANES:(b + 1) * LANES].astype(BF)
    finish(packed3, ROWS[2])
    sums[0].s5()
    sums[1].s3()
    sums[2].s0()

    for z in range(Z):
        for a in range(LAT):
            k = z * LAT + a
            base = (a // WLAT) * WIN + z * WLAT * WLON + (a % WLAT) * WLON
            rows_in[HALF * k:HALF * k + HALF, :] = grad_rows[base + HALF:base + WLON, :]
            xs[WLON * k + HALF:WLON * k + WLON, :] = grad_rows[base:base + HALF, :]
    fgrad_out[...] = rows_in[0:Z * LAT * HALF, :].astype(BF)
    edges.append(edge(3, fgrad_out, fgrad_in, east_of))

    s_table[...] = jnp.zeros_like(s_table)

    def added(blocks):
        lefts, hots = [], []
        for digit, hot, ds in blocks:
            hots.append(hot)
            lefts.append(jnp.concatenate(
                [jnp.where(digit == d, ds, 0.0) for d in range(DIGITS)], axis=0
            ).astype(BF))
        s_table[...] += dot(
            jnp.concatenate(lefts, axis=1), jnp.concatenate(hots, axis=1), NT
        )

    def main_table(step, carry):
        blocks = []
        for u in range(UNROLL):
            pair = step * UNROLL + u
            ds = jnp.concatenate(
                [dscore[th_rows(2 * pair), :], dscore[th_rows(2 * pair + 1), :]], axis=1
            )
            blocks.append(main_position(pair) + (ds,))
        added(blocks)
        return carry

    def tail_table(step, carry):
        blocks = []
        for u in range(UNROLL):
            key = step * UNROLL + u
            ds = jnp.concatenate([dtail0[th_rows(key), :], dtail1[th_rows(key), :]], axis=1)
            blocks.append(tail_position(key) + (ds,))
        added(blocks)
        return carry

    steps = WIN // 2 // UNROLL
    lax.fori_loop(0, steps // 2, main_table, 0)
    sums[0].s6()
    sums[1].s4()
    sums[2].s1()
    lax.fori_loop(steps // 2, steps, main_table, 0)
    sums[1].s5()
    sums[2].s2()
    lax.fori_loop(0, TAIL // UNROLL, tail_table, 0)
    for b in range(2):
        start = b * DIGITS * TH
        packed4[start:start + DIGITS * TH, :] = s_table[:, b * LANES:(b + 1) * LANES].astype(BF)
    finish(packed4, ROWS[3])
    sums[3].s0()
    sums[2].s3()

    edges[2].wait_recv()
    cts[0:Z * LAT // 2 * 3, :] = merged_in[...].astype(F32)
    for z in range(Z):
        for a in range(LAT // 2):
            k = z * (LAT // 2) + a
            ct_rows[8 * k:8 * k + 3, :] = cts[3 * k:3 * k + 3, :]
            merged_ref[z, a] = ct_rows[8 * k:8 * k + 6, :].astype(BF)
    sums[3].s1()
    sums[2].s4()
    edges[3].wait_recv()
    rows_in[0:Z * LAT * HALF, :] = fgrad_in[...].astype(F32)
    for z in range(Z):
        for a in range(LAT):
            k = z * LAT + a
            xs[WLON * k:WLON * k + HALF, :] = rows_in[HALF * k:HALF * k + HALF, :]
            fgrad_ref[z, a] = xs[WLON * k:WLON * k + WLON, :].astype(BF)
    sums[3].s2()
    sums[2].s5()
    sums[1].s6()
    sums[3].s3()
    sums[2].s6()
    sums[3].s4()
    sums[3].s5()
    sums[3].s6()
    for made in edges:
        made.wait_send()


def unpack_kernel(
    factor, merged_in, fgrad_in, sum1, sum2, sum3, sum4,
    merged_hbm, fgrad_hbm, qkv_hbm, proj_hbm, up_hbm, down_hbm, merge_hbm, table_hbm,
    qkv, proj, up, down, merge, table, sem,
):
    started = []

    def out(src, dst):
        made = pltpu.make_async_copy(src, dst, sem.at[len(started)])
        made.start()
        started.append(made)

    out(merged_in, merged_hbm)
    out(fgrad_in, fgrad_hbm)

    def scaled(ref, start, rows):
        return ref[start:start + rows, :].astype(F32) * factor

    for b in range(3):
        merge[:, b * LANES:(b + 1) * LANES] = scaled(sum1, b * 4 * C, 4 * C)
    out(merge, merge_hbm)
    down[:, 0:LANES] = scaled(sum2, 0, MLP)
    rest = scaled(sum2, MLP, MLP // 2)
    down[0:MLP // 2, LANES:] = rest[:, 0:C - LANES]
    down[MLP // 2:, LANES:] = rest[:, C - LANES:]
    out(down, down_hbm)
    for b in range(6):
        up[:, b * LANES:(b + 1) * LANES] = scaled(sum2, 6 * C + b * C, C)
    out(up, up_hbm)
    front = jnp.concatenate([scaled(sum3, b * C, C) for b in range(6)], axis=1)
    qkv[...] = front[:, :3 * C]
    out(qkv, qkv_hbm)
    proj[...] = front[:, 3 * C:]
    out(proj, proj_hbm)
    for b in range(2):
        for d in range(DIGITS):
            at = d * RADIX + b * LANES
            width = min(LANES, BPOS - at)
            block = scaled(sum4, (b * DIGITS + d) * TH, TH)
            for t in range(TYPES):
                table[t, :, at:at + width] = block[t * HEADS:(t + 1) * HEADS, :width]
    out(table, table_hbm)
    for made in started:
        made.wait()


def group_order():
    order = np.zeros((4 * GPAD, WIN), np.float32)
    for pa in range(2):
        for pb in range(2):
            for z in range(WZ):
                for a in range(WLAT // 2):
                    for b in range(WLON // 2):
                        cell = (z * (WLAT // 2) + a) * (WLON // 2) + b
                        token = (z * WLAT + 2 * a + pa) * WLON + 2 * b + pb
                        order[(2 * pa + pb) * GPAD + cell, token] = 1.0
    return jnp.asarray(order, BF)


def local(
    fields, norm_gain, qkv_weight, proj_weight, bias_table, bias_index, region_ids,
    mlp_gain, up_weight, down_weight, merge_gain, merge_weight, cotangent,
):
    n = lax.axis_size("lon")
    assert fields.shape[2] == WLON
    slow, fast = grid_sides(n)
    rows_of = piece_rows(n)
    gains = jnp.concatenate([norm_gain, mlp_gain, merge_gain]).reshape(6, C)
    tail_index = jnp.pad(
        bias_index[:, LANES:].T, ((0, 0), (0, RADIX - WIN)), constant_values=-1
    )
    labels = region_ids.reshape(WZ, TYPES, WLAT).transpose(1, 0, 2).reshape(TYPES, WZ * WLAT)
    labels = jnp.repeat(labels, WLON, axis=1)
    label_q = jnp.pad(labels, ((0, 0), (0, RADIX - WIN)), constant_values=-1)
    label_k = jnp.concatenate(
        [labels[:, :LANES]] + [labels[:, LANES:]] * HEADS
        + [jnp.full((TYPES, LANES - HEADS * TAIL), -2, labels.dtype)], axis=1,
    )
    labels = jnp.concatenate([label_q, label_k], axis=0)

    copies = 2 + 2 * (fast - 1) + 2 * (slow - 1)
    sums_scratch = [pltpu.VMEM((r, LANES), BF) for r in rows_of]
    sums_scratch += [pltpu.VMEM((r // 2, LANES), BF) for r in rows_of]
    sums_scratch += [pltpu.VMEM((r // 2, LANES), BF) for r in rows_of]
    sums_scratch += [pltpu.VMEM((fast - 1, r // (2 * fast), LANES), BF) for r in rows_of]
    sums_scratch += [pltpu.VMEM((r // (2 * fast), LANES), BF) for r in rows_of]
    sums_scratch += [pltpu.VMEM((slow - 1, r // n, LANES), BF) for r in rows_of]
    sums_scratch += [pltpu.SemaphoreType.DMA((copies,))] * 8
    halves = Z * LAT * HALF
    quarters = Z * LAT // 2 * 3
    outs = pl.pallas_call(
        functools.partial(block_kernel, n),
        out_shape=(
            jax.ShapeDtypeStruct(cotangent.shape, BF),
            jax.ShapeDtypeStruct(fields.shape, BF),
        ) + tuple(jax.ShapeDtypeStruct((r, LANES), BF) for r in rows_of),
        in_specs=[VMEM] * 4 + [ANY] * 9,
        out_specs=(VMEM,) * 6,
        scratch_shapes=[
            pltpu.VMEM(fields.shape, BF),
            pltpu.VMEM((Z, LAT, 8, C), BF),
            pltpu.VMEM(cotangent.shape, BF),
            pltpu.VMEM(cotangent.shape, BF),
            pltpu.VMEM(bias_table.shape, F32),
            pltpu.VMEM(bias_index.shape, jnp.int32),
            pltpu.VMEM(qkv_weight.shape, BF),
            pltpu.VMEM(proj_weight.shape, BF),
            pltpu.VMEM(up_weight.shape, BF),
            pltpu.VMEM(down_weight.shape, BF),
            pltpu.VMEM(merge_weight.shape, BF),
            pltpu.SemaphoreType.DMA((9,)),
            pltpu.SemaphoreType.DMA((4,)),
            pltpu.SemaphoreType.DMA((4,)),
            pltpu.VMEM((quarters, 2 * C), BF),
            pltpu.VMEM((quarters, 2 * C), BF),
            pltpu.VMEM((halves, C), BF),
            pltpu.VMEM((halves, C), BF),
        ] + sums_scratch + [
            pltpu.VMEM((WIN, LANES), jnp.int32),
            pltpu.VMEM((Z * LAT * 16, C), F32),
            pltpu.VMEM((Z * LAT // 2 * 8, 2 * C), F32),
            pltpu.VMEM((TOK, C), F32),
            pltpu.VMEM((TYPES * GPAD, 2 * C), F32),
            pltpu.VMEM((DIGITS * TH, RADIX), F32),
            pltpu.VMEM((3 * C, C), BF),
            pltpu.VMEM((WIN * TH, LANES), F32),
            pltpu.VMEM((TAIL * TH, LANES), F32),
            pltpu.VMEM((TAIL * TH, LANES), F32),
            pltpu.VMEM((LANES, RADIX), F32),
            pltpu.VMEM((C, C), BF),
            pltpu.VMEM((C, WIDE), BF),
            pltpu.VMEM((C, WIDE), BF),
            pltpu.VMEM((WIDE, C), BF),
            pltpu.VMEM((WIN, WIDE), F32),
            pltpu.VMEM((TYPES, WIN, WIDE), F32),
            pltpu.VMEM((TYPES, WIN, WIDE), BF),
            pltpu.VMEM((DIGITS * TH, WIDE), BF),
            pltpu.VMEM((WIN * TH, LANES), F32),
            pltpu.VMEM((TAIL * TH, LANES), F32),
            pltpu.VMEM((TAIL * TH, LANES), F32),
            pltpu.VMEM((RADIX, LANES), F32),
            pltpu.VMEM((TYPES, 3 * C, WIN), BF),
            pltpu.VMEM((TOK, C), BF),
            pltpu.VMEM((TOK, C), BF),
            pltpu.VMEM((TOK, C), BF),
            pltpu.VMEM((TOK, C), BF),
            pltpu.VMEM((TOK, MLP), F32),
            pltpu.VMEM((TOK, MLP), BF),
            pltpu.VMEM((TOK, C), BF),
            pltpu.VMEM((4, TYPES * GPAD, C), BF),
            pltpu.VMEM((TYPES * GPAD, 2 * C), BF),
            pltpu.VMEM((TOK, MLP), BF),
            pltpu.VMEM((TOK, C), BF),
            pltpu.VMEM((TOK, C), BF),
            pltpu.VMEM((TYPES, 3 * C, WIN), BF),
            pltpu.VMEM((TOK, C), F32),
            pltpu.VMEM((TYPES * GPAD, 2 * C), F32),
            pltpu.VMEM((DIGITS * TH, RADIX), F32),
        ],
        compiler_params=pltpu.CompilerParams(
            collective_id=0, has_side_effects=True, vmem_limit_bytes=56 << 20
        ),
        cost_estimate=pl.CostEstimate(
            flops=30_000_000_000, bytes_accessed=8 << 20, transcendentals=2_000_000
        ),
        name="block",
    )(
        gains, tail_index, labels, group_order(),
        fields, cotangent, bias_table, bias_index, qkv_weight, proj_weight,
        up_weight, down_weight, merge_weight,
    )

    factor = float(Z * LAT * fields.shape[2] * n) ** (-0.5)
    shapes = ((C, 3 * C), (C, C), (C, MLP), (MLP, C), (4 * C, 2 * C), (TYPES, HEADS, BPOS))
    return pl.pallas_call(
        functools.partial(unpack_kernel, factor),
        out_shape=(
            jax.ShapeDtypeStruct(cotangent.shape, BF),
            jax.ShapeDtypeStruct(fields.shape, BF),
        ) + tuple(jax.ShapeDtypeStruct(s, F32) for s in shapes),
        in_specs=[VMEM] * 6,
        out_specs=(ANY,) * 8,
        scratch_shapes=[pltpu.VMEM(s, F32) for s in shapes] + [pltpu.SemaphoreType.DMA((8,))],
        compiler_params=pltpu.CompilerParams(vmem_limit_bytes=16 << 20),
        cost_estimate=pl.CostEstimate(
            flops=1_000_000_000, bytes_accessed=6 << 20, transcendentals=0
        ),
        name="unpack",
    )(*outs)


def solution(mesh):
    grid = P("groups", None, "lon", None)
    rows = P("groups", None)
    return jax.shard_map(
        local,
        mesh=mesh,
        in_specs=(grid,) + (P(),) * 11 + (grid,),
        out_specs=(grid, grid) + (rows,) * 5 + (P("groups", None, None),),
        check_vma=False,
    )
```

time: 133 us -> 102 us (0.77)
  the two profiles are of different devices: /device:TPU:27 before, /device:TPU:0 now
where the time goes in v1:
time: 102 us
  Pallas kernels  81.7 us (80%)
  local copies, waits for them, and re-layouts  18.7 us (18%)
    pallas_call x1, Pallas kernels, local(): pl.pallas_call(functools.partial(block_kernel, n), out_shape=(jax.ShapeDt...  79.7 us
    unnamed x21, local copies, waits for them, and re-layouts  11.1 us
    pallas_call x4, local copies, waits for them, and re-layouts, local(): pl.pallas_call(functools.partial(unpack_kernel, factor), out_shape=(jax.S...  3.44 us

profile of v1, /device:TPU:0, one launch (start us, length us, event | category | flops | bytes accessed | tf_op | source)
XLA Modules:
  0.0 101.7 jit_solution(11827791663094808596)
XLA Ops:
  0.7 0.8 reshape.29
  1.5 0.1 reshape.30
  1.6 0.8 concatenate.10
  2.4 0.7 reshape.28.gains_ref
  3.2 0.1 concatenate.11
  3.3 0.6 select_add_fusion.labels_ref
  3.9 0.9 slice.8
  4.9 0.6 pad.8.tail_index_ref
  5.5 1.6 %copy.35.ct_hbm = bf16[2,12,6,384]{3,2,1,0:T(8,128)(2,1)} copy(bf16[2,12,6,384]{3,0,2,1:T(2,128)(2,1)} %param.26) | data formatting | bytes 221184 | tf_op args[12]
  7.1 1.8 %copy.34.fields_hbm = bf16[2,24,12,192]{3,2,1,0:T(8,128)(2,1)} copy(bf16[2,24,12,192]{3,1,2,0:T(8,128)(2,1)} %param.14) | data formatting | bytes 442368 | tf_op args[0]
  8.9 0.9 copy.37.wdown_hbm
  9.8 0.8 copy.36.table_hbm
  10.6 79.7 %block.1 = (bf16[2,12,6,384]{3,2,1,0:T(8,128)(2,1)}, bf16[2,24,12,192]{3,2,1,0:T(8,128)(2,1)}, bf16[2304,128]{1,0:T(8,128)(2,1)}, bf16[2304,128]{1,0:T(8,128)(2,...) custom-call(f32[6,192]{1,0:T(8,128)} %reshape.28.gains_ref, s32[16,256]{1,0:T(8,128)} %pad.8.tail_index_ref, ...), custom_call_target="tpu_custom_call" | custom-call | flops 30000001024 | bytes 8388608 | tf_op jit(solution)/shard_map/block/pallas_call | solution.py:752
  90.3 1.1 %copy-done = bf16[2304,128]{1,0:T(8,128)(2,1)S(1)} copy-done((bf16[2304,128]{1,0:T(8,128)(2,1)S(1)}, bf16[2304,128]{1,0:T(8,128)(2,1)}, u32[]{:S(2)}) %copy-start) | copy-done | bytes 589848
  91.4 1.1 %copy-done.1 = bf16[2304,128]{1,0:T(8,128)(2,1)S(1)} copy-done((bf16[2304,128]{1,0:T(8,128)(2,1)S(1)}, bf16[2304,128]{1,0:T(8,128)(2,1)}, u32[]{:S(2)}) %copy-start.1) | copy-done | bytes 589848
  92.5 1.0 copy-done.2
  93.4 1.0 copy-done.3
  94.4 0.9 copy-done.4
  95.3 0.9 copy-done.5
  96.3 2.0 %unpack.1 = (bf16[2,12,6,384]{3,2,1,0:T(8,128)(2,1)S(1)}, bf16[2,24,12,192]{3,2,1,0:T(8,128)(2,1)S(1)}, f32[192,576]{1,0:T(8,128)}, f32[192,192]{1,0:T(8,128)}, ...) custom-call(bf16[2,12,6,384]{3,2,1,0:T(8,128)(2,1)S(1)} %copy-done.5, ...), custom_call_target="tpu_custom_call" | custom-call | flops 1000000000 | bytes 6291456 | tf_op jit(solution)/shard_map/unpack/pallas_call | solution.py:836
  98.3 0.7 copy.38
  99.0 0.8 copy.39
  99.8 0.8 copy.41
  100.6 1.1 %copy.40 = f32[768,192]{0,1:T(8,128)} copy(f32[768,192]{1,0:T(8,128)S(1)} %get-tuple-element.33) | data formatting | bytes 1179648 | tf_op jit(solution)/shard_map/unpack/pallas_call | solution.py:836
  (16 shorter events, 0.2 us)
Async XLA Ops:
  0.6 8.2 %copy-start.7 = (bf16[768,192]{0,1:T(8,128)(2,1)S(1)}, bf16[768,192]{0,1:T(8,128)(2,1)}, u32[]{:S(2)}) copy-start(bf16[768,192]{0,1:T(8,128)(2,1)} %param.23) | copy-start | bytes 884740
  0.6 9.1 %copy-start.6 = (f32[4,6,3312]{2,0,1:T(4,128)S(1)}, f32[4,6,3312]{2,0,1:T(4,128)}, u32[]{:S(2)}) copy-start(f32[4,6,3312]{2,0,1:T(4,128)} %param.18) | copy-start | bytes 953860
  90.3 1.1 %copy-start = (bf16[2304,128]{1,0:T(8,128)(2,1)S(1)}, bf16[2304,128]{1,0:T(8,128)(2,1)}, u32[]{:S(2)}) copy-start(bf16[2304,128]{1,0:T(8,128)(2,1)} %get-tuple-element.16.sum1) | copy-start | bytes 1769476
  91.4 1.1 %copy-start.1 = (bf16[2304,128]{1,0:T(8,128)(2,1)S(1)}, bf16[2304,128]{1,0:T(8,128)(2,1)}, u32[]{:S(2)}) copy-start(bf16[2304,128]{1,0:T(8,128)(2,1)} %get-tuple-element.17.sum2) | copy-start | bytes 1769476
  92.5 1.0 copy-start.2
  93.4 1.0 copy-start.3
  94.4 0.9 copy-start.4
  95.3 0.9 copy-start.5
